TPU v7x, 32 devices: a whole 2x2x4 slice. The times are simulated.
32 devices in a mesh: groups: 2 (over y), range: 8 (over z, x), sub: 2 (over core).
Axes of the slice: x: 2, y: 2, z: 4, core: 2. Of those that a mesh axis runs over, the one named last changes fastest.
Arguments:
- samples: float32 [2, 1024, 32, 128], P(None, ('groups', 'range', 'sub')), parts along dimension 1, may hold values from -6 to 6
- beam_weights: float32 [32, 8, 2, 64, 128], P(('groups', 'range'), None, None, None, 'sub'), parts along dimension 0, may hold values from -0.25 to 0.25
- subarrays: int32 [32, 8, 64], P(('groups', 'range', 'sub')), parts along dimension 0, may hold values from 0 to 511, as said below
- training: int32 [64], P(('groups', 'range', 'sub')), parts along dimension 0, may hold values 0 or 1
Outputs:
- covariance: float32 [32, 8, 64, 128], P(('groups', 'range', 'sub')), parts along dimension 0
- filtered: float32 [2, 128, 64, 128], P(None, None, ('groups', 'range', 'sub')), parts along dimension 2
- energy: float32 [256], P('groups'), parts along dimension 0
There are 2 independent parts, one for each index of `groups`. A program takes and returns all parts, laid end to end along the dimension named above; each array names one. Nothing has to cross between parts.
Inputs may be any that keep to these rules, and one draw needn't show every extreme that they name: `subarrays`: in each gate block the 512 indices are all 512 channels, each once.
All inputs are finite; a program needn't handle non-finite values. No bound on the sum of `training` on one device may be relied on, other than what follows from the above.
Results may differ from a plain program's by a relative error of at most 0.0003.
Values sent between devices are 32-bit elements; how exact they have to be, the bound alone decides.
A program may use at most 64 MiB of HBM per device.

v0:
```python
import jax
import jax.numpy as jnp
from jax import lax
from jax.sharding import PartitionSpec as P

GB = 2
loading = 0.05


def block_terms(snaps, chosen, weights, masked, factor):
    highest = lax.Precision.HIGHEST
    picked = jnp.take(snaps, chosen, axis=1)
    real_part = picked[0]
    imag_part = picked[1]
    real_masked = real_part * masked
    imag_masked = imag_part * masked
    cov_real = (
        jnp.einsum("snx,smx->snm", real_masked, real_part, precision=highest)
        + jnp.einsum("snx,smx->snm", imag_masked, imag_part, precision=highest)
    ) * factor
    cov_imag = (
        jnp.einsum("snx,smx->snm", imag_masked, real_part, precision=highest)
        - jnp.einsum("snx,smx->snm", real_masked, imag_part, precision=highest)
    ) * factor
    w_real = weights[:, 0]
    w_imag = weights[:, 1]
    out_real = jnp.einsum("snk,snx->kx", w_real, real_part, precision=highest) + jnp.einsum(
        "snk,snx->kx", w_imag, imag_part, precision=highest
    )
    out_imag = jnp.einsum("snk,snx->kx", w_real, imag_part, precision=highest) - jnp.einsum(
        "snk,snx->kx", w_imag, real_part, precision=highest
    )
    prod_real = jnp.einsum("snm,smk->snk", cov_real, w_real, precision=highest) - jnp.einsum(
        "snm,smk->snk", cov_imag, w_imag, precision=highest
    )
    prod_imag = jnp.einsum("snm,smk->snk", cov_real, w_imag, precision=highest) + jnp.einsum(
        "snm,smk->snk", cov_imag, w_real, precision=highest
    )
    quadratic = jnp.sum(w_real * prod_real + w_imag * prod_imag, axis=(0, 1))
    inverse = 1.0 / jnp.sqrt(quadratic + loading)
    filtered = jnp.stack([out_real * inverse[:, None], out_imag * inverse[:, None]])
    energy = jnp.sum(out_real * out_real + out_imag * out_imag, axis=1)
    covariance = jnp.concatenate([cov_real, cov_imag], axis=-1)
    return (covariance, filtered, energy)


def body(samples, beam_weights, subarrays, training):
    range_count = lax.axis_size("range")
    core_count = lax.axis_size("sub")
    parts_iq, chan_dev, all_gates, pulses = samples.shape
    gate_dev = all_gates // (range_count * core_count)
    channels = chan_dev * range_count * core_count
    blocks_dev = gate_dev // GB
    spread = samples.reshape(parts_iq, 1, 1, chan_dev, range_count, core_count, gate_dev, pulses)
    turned = lax.all_to_all(
        lax.all_to_all(spread, "range", split_axis=4, concat_axis=1, tiled=True),
        "sub",
        split_axis=5,
        concat_axis=2,
        tiled=True,
    )
    local_data = turned.reshape(parts_iq, channels, blocks_dev, GB * pulses).transpose(2, 0, 1, 3)
    mine = lax.all_to_all(beam_weights, "sub", split_axis=0, concat_axis=4, tiled=True)
    gates_on = training.astype(jnp.float32).reshape(blocks_dev, GB)
    masked = jnp.repeat(gates_on, pulses, axis=1)
    factor = 1.0 / (GB * pulses)
    covs, filts, energies = jax.vmap(block_terms, in_axes=(0, 0, 0, 0, None))(
        local_data, subarrays, mine, masked, factor
    )
    beams = filts.shape[2]
    filtered = filts.reshape(blocks_dev, parts_iq, beams, GB, pulses).transpose(1, 2, 0, 3, 4)
    filtered = filtered.reshape(parts_iq, beams, gate_dev, pulses)
    total = lax.psum(jnp.sum(energies, axis=0), ("range", "sub"))
    energy = total / (all_gates * pulses)
    return (covs, filtered, energy)


def solution(mesh):
    placed = (
        P(None, ("groups", "range", "sub"), None, None),
        P(("groups", "range"), None, None, None, "sub"),
        P(("groups", "range", "sub"), None, None),
        P(("groups", "range", "sub")),
    )
    return jax.shard_map(
        body,
        mesh=mesh,
        in_specs=placed,
        out_specs=(
            P(("groups", "range", "sub"), None, None, None),
            P(None, None, ("groups", "range", "sub"), None),
            P("groups"),
        ),
        check_vma=False,
    )
```

profile of v0, /device:TPU:0, one launch (start us, length us, event | category | flops | bytes accessed | tf_op | source)
XLA Modules:
  0.0 92.5 jit_solution(9004139148378862796)
XLA Ops:
  0.6 0.0 copy-start
  0.6 2.5 %reshape.157 = f32[2,1,65536]{2,1,0:T(1,128)} reshape(f32[2,8,2,64,64]{4,3,2,1,0:T(8,128)} %param.5) | data formatting | bytes 1048576
  3.2 3.5 %all-to-all-start.2 = ((f32[2,1,65536]{2,1,0:T(1,128)}), f32[2,1,65536]{2,1,0:T(1,128)S(1)}, u32[]{:S(2)}, u32[]{:S(2)}) async-start(f32[2,1,65536]{2,1,0:T(1,128)} %reshape.157), calls=%async_computation.2 | async-start | bytes 1048576 | tf_op jit(solution)/shard_map/all_to_all | solution.py:63
  6.6 0.0 copy-done
  6.7 1.6 %copy.24 = f32[2,1,1,32,8,2,2,128]{7,6,3,5,0,2,1,4:T(2,128)} copy(f32[2,1,1,32,8,2,2,128]{7,6,5,4,3,0,2,1:T(2,128)S(1)} %bitcast.103) | data formatting | bytes 2097152 | tf_op jit(solution)/shard_map/reshape | solution.py:54
  8.2 0.0 copy-start.2
  8.2 0.2 all-to-all-done.2
  8.4 0.0 copy-start.1
  8.4 7.4 %all-to-all-start = ((f32[2,1,1,32,8,2,2,128]{7,6,3,5,0,2,1,4:T(2,128)}), f32[2,1,1,32,8,2,2,128]{7,6,3,5,0,2,1,4:T(2,128)S(1)}, u32[]{:S(2)}, u32[]{:S(2)}) async-start(f32[2,1,1,32,8,2,2,128]{7,6,3,5,0,2,1,4:T(2,128)} %copy.24), calls=%async_computation | async-start | bytes 2097152 | tf_op jit(solution)/shard_map/all_to_all | solution.py:56
  15.8 0.0 copy-done.2
  15.8 0.0 copy-done.1
  15.9 0.1 reshape.147
  15.9 0.5 broadcast.75
  16.4 2.3 %reduce.5 = f32[2,65536]{1,0:T(2,128)S(1)} reduce(f32[2,1,65536]{2,1,0:T(1,128)S(1)} %all-to-all-done.2, f32[]{:T(128)} %broadcast.75), dimensions={1}, to_apply=%all_to_all.44.reduce_sub_computation | reduce | bytes 1048580 | tf_op jit(solution)/shard_map/all_to_all | solution.py:63
  18.8 0.6 reshape.158
  19.4 1.9 %copy.29 = f32[1,8,2,64,2,64]{5,4,3,1,2,0:T(2,128)} copy(f32[1,8,2,64,2,64]{5,3,2,1,4,0:T(8,128)S(1)} %bitcast.98) | data formatting | bytes 1048576 | tf_op jit(solution)/shard_map/all_to_all | solution.py:63
  21.2 1.8 %all_to_all.47 = f32[1,8,2,64,128]{4,3,1,2,0:T(8,128)S(1)} reshape(f32[1,8,2,64,2,64]{5,4,3,1,2,0:T(2,128)} %copy.29) | data formatting | bytes 1048576 | tf_op jit(solution)/shard_map/all_to_all | solution.py:63
  23.1 0.1 broadcast_bitcast_fusion
  23.1 18.9 %all-to-all-done = f32[2,1,1,32,8,2,2,128]{7,6,3,5,0,2,1,4:T(2,128)S(1)} async-done(((f32[2,1,1,32,8,2,2,128]{7,6,3,5,0,2,1,4:T(2,128)}), f32[2,1,1,32,8,2,2,128]{7,6,3,5,0,2,1,4:T(2,128)S(1)}, u32[]{:S(2)}, u32[]{:S(2)}) %all-to-all-start) | async-done | bytes 1048608 | tf_op jit(solution)/shard_map/all_to_all | solution.py:56
  42.1 0.1 copy.25
  42.1 4.6 %all_to_all.51 = f32[2,8,1,32,1,2,2,128]{7,6,3,1,0,4,2,5:T(2,128)S(1)} all-to-all(f32[2,8,1,32,1,2,2,128]{7,6,3,1,0,4,2,5:T(2,128)S(1)} %copy.25), channel_id=1, replica_groups=mesh['groups'=2,'range'=8,'sub'=2] {'sub'}, dimensions={5} | all-to-all | bytes 2097152 | tf_op jit(solution)/shard_map/all_to_all | solution.py:55
  46.7 0.1 copy.26
  46.8 0.8 copy.27
  47.6 2.3 %gather_fusion = f32[512,2,256]{2,1,0:T(2,128)S(1)} fusion(f32[1,2,512,256]{3,1,2,0:T(2,128)S(1)} %copy.27, s32[512]{0:T(512)S(1)} %reshape.147), kind=kCustom, calls=%fused_computation | custom fusion | bytes 2101248 | tf_op jit(solution)/shard_map/vmap(jit(_take))/gather | solution.py:12
  50.0 0.1 copy.28
  50.1 0.1 broadcast_select_fusion
  50.2 1.0 %convolution_bitcast_fusion.2 = f32[256,128]{1,0:T(8,128)S(1)} fusion(f32[1,2,8,64,256]{4,3,2,1,0:T(8,128)S(1)} %broadcast_select_fusion, f32[1,8,2,64,128]{4,3,1,2,0:T(8,128)S(1)} %all_to_all.47), kind=kOutput, calls=%fused_computation.13 | convolution fusion | flops 201326592 | bytes 917504 | tf_op jit(solution)/shard_map/vmap(snk,snx->kx)/dot_general | solution.py:27
  51.2 1.0 %convolution_bitcast_fusion = f32[256,128]{1,0:T(8,128)S(1)} fusion(f32[1,2,8,64,256]{4,3,2,1,0:T(8,128)S(1)} %broadcast_select_fusion, f32[1,8,2,64,128]{4,3,1,2,0:T(8,128)S(1)} %all_to_all.47), kind=kOutput, calls=%fused_computation.11 | convolution fusion | flops 201326592 | bytes 917504 | tf_op jit(solution)/shard_map/vmap(snk,snx->kx)/dot_general | solution.py:30
  52.2 0.6 fusion.12
  52.9 0.6 fusion.2
  53.5 0.4 fusion.19
  53.9 0.4 fusion.18
  54.3 0.6 fusion.8
  54.9 1.0 %fusion.6 = f32[256,128]{1,0:T(8,128)S(1)} fusion(f32[256,128]{1,0:T(8,128)S(1)} %convolution_bitcast_fusion.2, f32[1,2,8,64,256]{4,3,2,1,0:T(8,128)S(1)} %broadcast_select_fusion, f32[1,8,2,64,128]{4,3,1,2,0:T(8,128)S(1)} %all_to_all.47), kind=kOutput, calls=%fused_computation.15 | convolution fusion | flops 201359360 | bytes 1048576 | tf_op jit(solution)/shard_map/vmap(snk,snx->kx)/dot_general | solution.py:27
  55.9 0.6 fusion.3
  56.5 0.4 fusion
  56.9 0.4 fusion.5
  57.4 1.0 %add_reduce_fusion = (f32[128]{0:T(128)S(1)}, f32[256,128]{1,0:T(8,128)S(1)}, f32[256,128]{1,0:T(8,128)S(1)}) fusion(f32[256,128]{1,0:T(8,128)S(1)} %fusion.6, f32[128]{0:T(128)S(1)} %add_rsqrt_fusion, f32[256,128]{1,0:T(8,128)S(1)} %convolution_bitcast_fusion, f32[1,8,2,64,128]{4,3,1,2,0:T(8,128)S(1)} %all_to_all.47, ...), kind=kOutput, calls=%fused_computation.36 | convolution fusion | flops 201555840 | bytes 1311744 | tf_op jit(solution)/shard_map/vmap(snk,snx->kx)/dot_general | solution.py:30
  58.4 31.6 %psum.7 = f32[128]{0:T(128)S(1)} all-reduce(f32[128]{0:T(128)S(1)} %get-tuple-element.3), channel_id=1, replica_groups=mesh['groups'=2,'range'=8,'sub'=2] {'range','sub'}, use_global_device_ids=true, to_apply=%region_2.3 | all-reduce | flops 128 | bytes 1024 | tf_op jit(solution)/shard_map/psum | solution.py:73
  90.1 0.5 broadcast_multiply_fusion.2
  90.6 0.1 copy.30
  90.7 0.1 copy.31
  90.8 0.8 pad_maximum_fusion
  91.7 0.8 pad_maximum_fusion.1
  (6 shorter events, 0.0 us)
Async XLA Ops:
  0.6 6.0 %copy-start = (f32[2,32,32,128]{3,2,1,0:T(8,128)S(1)}, f32[2,32,32,128]{3,2,1,0:T(8,128)}, u32[]{:S(2)}) copy-start(f32[2,32,32,128]{3,2,1,0:T(8,128)} %param.4) | copy-start | bytes 3145732
  3.2 5.2 %all-to-all-start.2 = ((f32[2,1,65536]{2,1,0:T(1,128)}), f32[2,1,65536]{2,1,0:T(1,128)S(1)}, u32[]{:S(2)}, u32[]{:S(2)}) async-start(f32[2,1,65536]{2,1,0:T(1,128)} %reshape.157), calls=%async_computation.2 | async-start | bytes 1048576 | tf_op jit(solution)/shard_map/all_to_all | solution.py:63
  8.2 7.6 %copy-start.2 = (s32[2]{0:T(128)S(1)}, s32[2]{0:T(128)}, u32[]{:S(2)}) copy-start(s32[2]{0:T(128)} %param.7) | copy-start | bytes 28
  8.4 7.4 %copy-start.1 = (s32[1,8,64]{2,1,0:T(8,128)S(1)}, s32[1,8,64]{2,1,0:T(8,128)}, u32[]{:S(2)}) copy-start(s32[1,8,64]{2,1,0:T(8,128)} %param.6) | copy-start | bytes 6148
  8.4 33.7 %all-to-all-start = ((f32[2,1,1,32,8,2,2,128]{7,6,3,5,0,2,1,4:T(2,128)}), f32[2,1,1,32,8,2,2,128]{7,6,3,5,0,2,1,4:T(2,128)S(1)}, u32[]{:S(2)}, u32[]{:S(2)}) async-start(f32[2,1,1,32,8,2,2,128]{7,6,3,5,0,2,1,4:T(2,128)} %copy.24), calls=%async_computation | async-start | bytes 2097152 | tf_op jit(solution)/shard_map/all_to_all | solution.py:56
where the time goes:
time: 92.9 us; the launch traced here: 92.5 us
  blocking collectives  36.2 us (39%)
  waiting for transfers between devices  19.1 us (21%)
  local copies, waits for them, and re-layouts  12.7 us (14%)
  starting transfers between devices  10.9 us (12%)
  matrix products  8.13 us (9%)
  other arithmetic  4.67 us (5%)
    psum x1, blocking collectives, body(): total = lax.psum(jnp.sum(energies, axis=0), ('range', 'sub'))  31.6 us
    all_to_all x1, waiting for transfers between devices, body(): lax.all_to_all(spread, 'range', split_axis=4, concat_axis=1, tiled=True)  18.9 us
    all_to_all x1, starting transfers between devices, body(): lax.all_to_all(spread, 'range', split_axis=4, concat_axis=1, tiled=True)  7.41 us
    all_to_all x1, blocking collectives, body(): lax.all_to_all(lax.all_to_all(spread, 'range', split_axis=4, concat_axis=...  4.58 us
    all_to_all x3, local copies, waits for them, and re-layouts, body(): lax.all_to_all(beam_weights, 'sub', split_axis=0, concat_axis=4, tiled=True)  4.18 us
    all_to_all x1, starting transfers between devices, body(): lax.all_to_all(beam_weights, 'sub', split_axis=0, concat_axis=4, tiled=True)  3.49 us
    unnamed x8, local copies, waits for them, and re-layouts  3.15 us
    gather x4, local copies, waits for them, and re-layouts, block_terms(): picked = jnp.take(snaps, chosen, axis=1)  2.5 us
  transfers between devices with their start and end apart: 2, of which 2 were waited for; matrix products, arithmetic and copies ran while one was open for 8% of the time, Pallas kernels for 0%

commit v1 on v0

--- a/solution.py
+++ b/solution.py
@@ -1,10 +1,22 @@
+import functools
 import jax
 import jax.numpy as jnp
 from jax import lax
 from jax.sharding import PartitionSpec as P
+from jax.lax import all_to_all, psum
 
 GB = 2
 loading = 0.05
+
+
+def lane_part(u_in, link_axis):
+    current_block = jnp.concatenate(
+        all_to_all(jnp.stack(jnp.split(u_in, psum(1, link_axis), axis=4)), link_axis, 0, 0), axis=1
+    )
+    return current_block
+
+
+supply_all_the_body = functools.partial(lane_part, link_axis="range")
 
 
 def block_terms(snaps, chosen, weights, masked, factor):
@@ -53,11 +65,7 @@
     blocks_dev = gate_dev // GB
     spread = samples.reshape(parts_iq, 1, 1, chan_dev, range_count, core_count, gate_dev, pulses)
     turned = lax.all_to_all(
-        lax.all_to_all(spread, "range", split_axis=4, concat_axis=1, tiled=True),
-        "sub",
-        split_axis=5,
-        concat_axis=2,
-        tiled=True,
+        supply_all_the_body(spread), "sub", split_axis=5, concat_axis=2, tiled=True
     )
     local_data = turned.reshape(parts_iq, channels, blocks_dev, GB * pulses).transpose(2, 0, 1, 3)
     mine = lax.all_to_all(beam_weights, "sub", split_axis=0, concat_axis=4, tiled=True)

time: 92.9 us -> 93.9 us (1.011)
  local copies, waits for them, and re-layouts: 12.7 us -> 14.2 us
    another operation x0 -> x2, local copies, waits for them, and re-layouts: none -> 1.82 us  [lane_part(): jnp.stack(jnp.split(u_in, psum(1, link_axis), axis=4))]
    reshape x1, local copies, waits for them, and re-layouts: 1.56 us -> 0.07 us  [lane_part(): jnp.concatenate(all_to_all(jnp.stack(jnp.split(u_in, psum(1, link_axis),...]
    unnamed x8 -> x16, local copies, waits for them, and re-layouts: 3.15 us -> 4.41 us
  transfers between devices with their start and end apart: 2 -> 2, of which waited for: 2 -> 1; matrix products, arithmetic and copies ran while one was open for 8% -> 9% of each run, Pallas kernels for 0% -> 0%
where the time goes in v1:
time: 93.9 us; the launch traced here: 93.5 us
  blocking collectives  36.2 us (39%)
  waiting for transfers between devices  18.5 us (20%)
  local copies, waits for them, and re-layouts  14.2 us (15%)
  starting transfers between devices  10.9 us (12%)
  matrix products  8.13 us (9%)
  other arithmetic  4.67 us (5%)
    psum x1, blocking collectives, body(): total = lax.psum(jnp.sum(energies, axis=0), ('range', 'sub'))  31.6 us
    all_to_all x1, waiting for transfers between devices, lane_part(): all_to_all(jnp.stack(jnp.split(u_in, psum(1, link_axis), axis=4)), link_a...  18.5 us
    all_to_all x1, starting transfers between devices, lane_part(): all_to_all(jnp.stack(jnp.split(u_in, psum(1, link_axis), axis=4)), link_a...  7.41 us
    all_to_all x1, blocking collectives, body(): lax.all_to_all(supply_all_the_body(spread), 'sub', split_axis=5, concat_a...  4.58 us
    unnamed x16, local copies, waits for them, and re-layouts  4.41 us
    all_to_all x3, local copies, waits for them, and re-layouts, body(): lax.all_to_all(beam_weights, 'sub', split_axis=0, concat_axis=4, tiled=True)  4.18 us
    all_to_all x1, starting transfers between devices, body(): lax.all_to_all(beam_weights, 'sub', split_axis=0, concat_axis=4, tiled=True)  3.49 us
    gather x4, local copies, waits for them, and re-layouts, block_terms(): picked = jnp.take(snaps, chosen, axis=1)  2.5 us
  transfers between devices with their start and end apart: 2, of which 1 were waited for; matrix products, arithmetic and copies ran while one was open for 9% of the time, Pallas kernels for 0%

profile of v1, /device:TPU:0, one launch (start us, length us, event | category | flops | bytes accessed | tf_op | source)
XLA Modules:
  0.0 93.5 jit_solution(8387221588690152034)
XLA Ops:
  0.6 0.0 copy-start
  0.6 2.5 %reshape.165 = f32[2,1,65536]{2,1,0:T(1,128)} reshape(f32[2,8,2,64,64]{4,3,2,1,0:T(8,128)} %param.5) | data formatting | bytes 1048576
  3.2 3.5 %all-to-all-start.2 = ((f32[2,1,65536]{2,1,0:T(1,128)}), f32[2,1,65536]{2,1,0:T(1,128)S(1)}, u32[]{:S(2)}, u32[]{:S(2)}) async-start(f32[2,1,65536]{2,1,0:T(1,128)} %reshape.165), calls=%async_computation.2 | async-start | bytes 1048576 | tf_op jit(solution)/shard_map/all_to_all | solution.py:71
  6.6 0.0 copy-done
  6.7 0.6 copy.37
  7.4 1.8 %copy.45 = f32[8,2,1,1,32,1,2,2,128]{8,7,4,6,1,5,3,2,0:T(2,128)} copy(f32[8,2,1,1,32,1,2,2,128]{8,4,7,6,1,5,3,2,0:T(8,128)S(1)} %fusion.20) | data formatting | bytes 2097152 | tf_op jit(solution)/shard_map/stack | solution.py:14
  9.2 0.0 copy-start.1
  9.2 0.0 all-to-all-done.2
  9.2 7.4 %all-to-all-start = ((f32[8,2,1,1,32,1,2,2,128]{8,7,4,6,1,5,3,2,0:T(2,128)}), f32[8,2,1,1,32,1,2,2,128]{8,7,4,6,1,5,3,2,0:T(2,128)S(1)}, u32[]{:S(2)}, u32[]{:S(2)}) async-start(f32[8,2,1,1,32,1,2,2,128]{8,7,4,6,1,5,3,2,0:T(2,128)} %copy.45), calls=%async_computation | async-start | bytes 2097152 | tf_op jit(solution)/shard_map/all_to_all | solution.py:14
  16.7 0.0 copy-done.1
  16.7 0.0 copy-start.2
  16.7 0.1 reshape.155
  16.8 0.6 copy-done.2
  17.4 0.5 broadcast.75
  17.9 2.3 %reduce.5 = f32[2,65536]{1,0:T(2,128)S(1)} reduce(f32[2,1,65536]{2,1,0:T(1,128)S(1)} %all-to-all-done.2, f32[]{:T(128)} %broadcast.75), dimensions={1}, to_apply=%all_to_all.31.reduce_sub_computation | reduce | bytes 1048580 | tf_op jit(solution)/shard_map/all_to_all | solution.py:71
  20.2 0.6 reshape.166
  20.8 1.9 %copy.50 = f32[1,8,2,64,2,64]{5,4,3,1,2,0:T(2,128)} copy(f32[1,8,2,64,2,64]{5,3,2,1,4,0:T(8,128)S(1)} %bitcast.150) | data formatting | bytes 1048576 | tf_op jit(solution)/shard_map/all_to_all | solution.py:71
  22.7 1.8 %all_to_all.34 = f32[1,8,2,64,128]{4,3,1,2,0:T(8,128)S(1)} reshape(f32[1,8,2,64,2,64]{5,4,3,1,2,0:T(2,128)} %copy.50) | data formatting | bytes 1048576 | tf_op jit(solution)/shard_map/all_to_all | solution.py:71
  24.5 0.1 broadcast_bitcast_fusion
  24.6 18.5 %all-to-all-done = f32[8,2,1,1,32,1,2,2,128]{8,7,4,6,1,5,3,2,0:T(2,128)S(1)} async-done(((f32[8,2,1,1,32,1,2,2,128]{8,7,4,6,1,5,3,2,0:T(2,128)}), f32[8,2,1,1,32,1,2,2,128]{8,7,4,6,1,5,3,2,0:T(2,128)S(1)}, u32[]{:S(2)}, u32[]{:S(2)}) %all-to-all-start) | async-done | bytes 1048608 | tf_op jit(solution)/shard_map/all_to_all | solution.py:14
  43.1 0.1 copy.46
  43.1 4.6 %all_to_all.38 = f32[2,8,1,32,1,2,2,128]{7,6,3,1,0,4,2,5:T(2,128)S(1)} all-to-all(f32[2,8,1,32,1,2,2,128]{7,6,3,1,0,4,2,5:T(2,128)S(1)} %copy.46), channel_id=1, replica_groups=mesh['groups'=2,'range'=8,'sub'=2] {'sub'}, dimensions={5} | all-to-all | bytes 2097152 | tf_op jit(solution)/shard_map/all_to_all | solution.py:67
  47.7 0.1 copy.47
  47.8 0.8 copy.48
  48.6 2.3 %gather_fusion = f32[512,2,256]{2,1,0:T(2,128)S(1)} fusion(f32[1,2,512,256]{3,1,2,0:T(2,128)S(1)} %copy.48, s32[512]{0:T(512)S(1)} %reshape.155), kind=kCustom, calls=%fused_computation | custom fusion | bytes 2101248 | tf_op jit(solution)/shard_map/vmap(jit(_take))/gather | solution.py:24
  51.0 0.1 copy.49
  51.1 0.1 broadcast_select_fusion
  51.2 0.6 fusion.12
  51.9 0.6 fusion.8
  52.5 0.6 fusion.2
  53.1 0.4 fusion.19
  53.5 0.4 fusion.18
  53.9 1.0 %convolution_bitcast_fusion.2 = f32[256,128]{1,0:T(8,128)S(1)} fusion(f32[1,2,8,64,256]{4,3,2,1,0:T(8,128)S(1)} %broadcast_select_fusion, f32[1,8,2,64,128]{4,3,1,2,0:T(8,128)S(1)} %all_to_all.34), kind=kOutput, calls=%fused_computation.13 | convolution fusion | flops 201326592 | bytes 917504 | tf_op jit(solution)/shard_map/vmap(snk,snx->kx)/dot_general | solution.py:39
  54.9 1.0 %convolution_bitcast_fusion = f32[256,128]{1,0:T(8,128)S(1)} fusion(f32[1,2,8,64,256]{4,3,2,1,0:T(8,128)S(1)} %broadcast_select_fusion, f32[1,8,2,64,128]{4,3,1,2,0:T(8,128)S(1)} %all_to_all.34), kind=kOutput, calls=%fused_computation.11 | convolution fusion | flops 201326592 | bytes 917504 | tf_op jit(solution)/shard_map/vmap(snk,snx->kx)/dot_general | solution.py:42
  55.9 0.6 fusion.3
  56.6 0.4 fusion
  57.0 0.4 fusion.5
  57.4 1.0 %fusion.6 = f32[256,128]{1,0:T(8,128)S(1)} fusion(f32[256,128]{1,0:T(8,128)S(1)} %convolution_bitcast_fusion.2, f32[1,2,8,64,256]{4,3,2,1,0:T(8,128)S(1)} %broadcast_select_fusion, f32[1,8,2,64,128]{4,3,1,2,0:T(8,128)S(1)} %all_to_all.34), kind=kOutput, calls=%fused_computation.15 | convolution fusion | flops 201359360 | bytes 1048576 | tf_op jit(solution)/shard_map/vmap(snk,snx->kx)/dot_general | solution.py:39
  58.4 1.0 %add_reduce_fusion = (f32[128]{0:T(128)S(1)}, f32[256,128]{1,0:T(8,128)S(1)}, f32[256,128]{1,0:T(8,128)S(1)}) fusion(f32[256,128]{1,0:T(8,128)S(1)} %fusion.6, f32[128]{0:T(128)S(1)} %add_rsqrt_fusion, f32[256,128]{1,0:T(8,128)S(1)} %convolution_bitcast_fusion, f32[1,8,2,64,128]{4,3,1,2,0:T(8,128)S(1)} %all_to_all.34, ...), kind=kOutput, calls=%fused_computation.52 | convolution fusion | flops 201555840 | bytes 1311744 | tf_op jit(solution)/shard_map/vmap(snk,snx->kx)/dot_general | solution.py:42
  59.4 0.1 copy.51
  59.6 0.1 copy.52
  59.7 31.6 %psum.7 = f32[128]{0:T(128)S(1)} all-reduce(f32[128]{0:T(128)S(1)} %get-tuple-element.3), channel_id=1, replica_groups=mesh['groups'=2,'range'=8,'sub'=2] {'range','sub'}, use_global_device_ids=true, to_apply=%region_2.3 | all-reduce | flops 128 | bytes 1024 | tf_op jit(solution)/shard_map/psum | solution.py:81
  91.3 0.5 broadcast_multiply_fusion.2
  91.8 0.8 pad_maximum_fusion.1
  92.7 0.8 pad_maximum_fusion
  (14 shorter events, 0.1 us)
Async XLA Ops:
  0.6 6.0 %copy-start = (f32[2,32,32,128]{3,2,1,0:T(8,128)S(1)}, f32[2,32,32,128]{3,2,1,0:T(8,128)}, u32[]{:S(2)}) copy-start(f32[2,32,32,128]{3,2,1,0:T(8,128)} %param.4) | copy-start | bytes 3145732
  3.2 6.1 %all-to-all-start.2 = ((f32[2,1,65536]{2,1,0:T(1,128)}), f32[2,1,65536]{2,1,0:T(1,128)S(1)}, u32[]{:S(2)}, u32[]{:S(2)}) async-start(f32[2,1,65536]{2,1,0:T(1,128)} %reshape.165), calls=%async_computation.2 | async-start | bytes 1048576 | tf_op jit(solution)/shard_map/all_to_all | solution.py:71
  9.2 7.4 %copy-start.1 = (s32[1,8,64]{2,1,0:T(8,128)S(1)}, s32[1,8,64]{2,1,0:T(8,128)}, u32[]{:S(2)}) copy-start(s32[1,8,64]{2,1,0:T(8,128)} %param.6) | copy-start | bytes 6148
  9.2 33.8 %all-to-all-start = ((f32[8,2,1,1,32,1,2,2,128]{8,7,4,6,1,5,3,2,0:T(2,128)}), f32[8,2,1,1,32,1,2,2,128]{8,7,4,6,1,5,3,2,0:T(2,128)S(1)}, u32[]{:S(2)}, u32[]{:S(2)}) async-start(f32[8,2,1,1,32,1,2,2,128]{8,7,4,6,1,5,3,2,0:T(2,128)} %copy.45), calls=%async_computation | async-start | bytes 2097152 | tf_op jit(solution)/shard_map/all_to_all | solution.py:14
  16.7 0.7 copy-start.2
